TPU v7x, 32 devices: a whole 2x2x4 slice. The times are simulated.
32 devices in a mesh: leaf: 8 (over z, x), rhs: 4 (over y, core).
Axes of the slice: x: 2, y: 2, z: 4, core: 2. Of those that a mesh axis runs over, the one named last changes fastest.
Arguments:
- right_sides: bfloat16 [8192, 4096], P('leaf', 'rhs'), may hold values from -6 to 6
- leaf_inverse: bfloat16 [8192, 1024], P(('leaf', 'rhs')), may hold values from -0.1875 to 0.1875
- project_factors: bfloat16 [3, 8192, 128], P(None, 'leaf'), may hold values from -0.1875 to 0.1875
- correct_factors: bfloat16 [3, 8192, 128], P(None, 'leaf'), may hold values from -0.5 to 0.5
- coupling_first: bfloat16 [4, 256, 256], P(None, 'rhs'), may hold values from -0.375 to 0.375
- coupling_second: bfloat16 [2, 256, 256], P(None, 'rhs'), may hold values from -0.375 to 0.375
- coupling_third: bfloat16 [1, 256, 256], P(None, 'rhs'), may hold values from -0.375 to 0.375
Outputs:
- solution: bfloat16 [8192, 4096], P('leaf', 'rhs')
All inputs are finite; a program needn't handle non-finite values.
Results may differ from a plain program's by a relative error of at most 0.014.
Values may be sent and summed in bfloat16 or wider, within the bound.
A program may use at most 64 MiB of HBM per device.

v0:
```python
import jax
import jax.numpy as jnp
from jax import lax
from jax.sharding import PartitionSpec as P

LEVELS = 3


def from_partner(value, axis, stride):
    mask = 2**stride
    pairs = [(source, source ^ mask) for source in range(lax.axis_size(axis))]
    return lax.ppermute(value, axis, pairs)


def halve(part, bit, index):
    width = part.shape[1] // 2
    upper_side = index >> bit & 1 == 1
    lower = part[:, :width]
    higher = part[:, width:]
    outgoing = jnp.where(upper_side, lower, higher)
    kept = jnp.where(upper_side, higher, lower)
    return kept + from_partner(outgoing, "leaf", bit)


def regrow(part, bit, index):
    incoming = from_partner(part, "leaf", bit)
    upper_side = index >> bit & 1 == 1
    return jnp.where(
        upper_side, jnp.concatenate([incoming, part], 1), jnp.concatenate([part, incoming], 1)
    )


def couple(mine, theirs, coupling_rows, side):
    stacked = jnp.where(
        side == 0, jnp.concatenate([mine, theirs], 0), jnp.concatenate([theirs, mine], 0)
    )
    return jnp.dot(coupling_rows, stacked, preferred_element_type=jnp.float32).astype(jnp.bfloat16)


def local(
    right_sides,
    leaf_inverse,
    project_factors,
    correct_factors,
    coupling_first,
    coupling_second,
    coupling_third,
):
    index = lax.axis_index("leaf")
    rank = project_factors.shape[2]
    start_rows = jnp.dot(
        lax.all_gather(leaf_inverse, "rhs", axis=0, tiled=True),
        right_sides,
        preferred_element_type=jnp.float32,
    ).astype(jnp.bfloat16)
    current = start_rows.astype(jnp.float32)
    own_nodes = []
    for level, table in enumerate((coupling_first, coupling_second, coupling_third)):
        own_nodes.append(lax.dynamic_slice_in_dim(table, index >> level + 1, 1, 0)[0])
    gathered = (
        lax.all_gather(own_nodes[0], "rhs", axis=0, tiled=True),
        lax.all_gather(own_nodes[1], "rhs", axis=0, tiled=True),
        lax.all_gather(own_nodes[2], "rhs", axis=0, tiled=True),
    )
    for level in range(LEVELS):
        rounded = current.astype(jnp.bfloat16)
        projection = jnp.dot(project_factors[level].T, rounded, preferred_element_type=jnp.float32)
        side = index >> level & 1
        coupling_rows = lax.dynamic_slice_in_dim(gathered[level], side * rank, rank, 0)
        for bit in range(level):
            projection = halve(projection, bit, index)
        mine = projection.astype(jnp.bfloat16)
        theirs = from_partner(mine, "leaf", level)
        answer = couple(mine, theirs, coupling_rows, side)
        for bit in reversed(range(level)):
            answer = regrow(answer, bit, index)
        current = current - jnp.dot(
            correct_factors[level], answer, preferred_element_type=jnp.float32
        )
    return current.astype(jnp.bfloat16)


def solution(mesh):
    in_specs = (
        P("leaf", "rhs"),
        P(("leaf", "rhs"), None),
        P(None, "leaf", None),
        P(None, "leaf", None),
        P(None, "rhs", None),
        P(None, "rhs", None),
        P(None, "rhs", None),
    )
    out_specs = P("leaf", "rhs")
    return jax.shard_map(local, mesh=mesh, in_specs=in_specs, out_specs=out_specs, check_vma=False)
```

profile of v0, /device:TPU:0, one launch (start us, length us, event | category | flops | bytes accessed | tf_op | source)
XLA Modules:
  0.0 126.6 jit_solution(1204072495971982888)
XLA Ops:
  6.5 0.0 copy-start
  6.5 0.0 all-gather.5.cloned.1.call-start
  6.5 0.7 all-gather.5.cloned.1.call-update
  7.3 27.0 %all-gather.5.cloned.1.call-done = bf16[1024,1024]{1,0:T(8,128)(2,1)} async-done(((bf16[256,1024]{1,0:T(8,128)(2,1)}), bf16[1024,1024]{1,0:T(8,128)(2,1)}) %all-gather.5.cloned.1.call-update) | async-done | bytes 2097168 | tf_op jit(solution)/shard_map/all_gather | solution.py:52
  34.2 0.0 copy-done
  34.2 3.9 %convolution_convert_fusion = bf16[1024,1024]{1,0:T(8,128)(2,1)S(1)} fusion(bf16[1024,1024]{1,0:T(8,128)(2,1)} %all-gather.5.cloned.1.call-done, bf16[1024,1024]{1,0:T(8,128)(2,1)S(1)} %copy-done), kind=kOutput, calls=%fused_computation.8 | convolution fusion | flops 2148532224 | bytes 6291456 | tf_op jit(solution)/shard_map/dot_general | solution.py:51
  38.1 0.0 copy-start.2
  38.2 0.0 copy-start.4
  38.2 1.7 %fusion.12 = bf16[128,1024]{1,0:T(8,128)(2,1)S(1)} fusion(bf16[1024,1024]{1,0:T(8,128)(2,1)S(1)} %convolution_convert_fusion, bf16[3,1024,128]{2,1,0:T(8,128)(2,1)} %param.9), kind=kOutput, calls=%fused_computation.13 | convolution fusion | flops 268566528 | bytes 2621440 | tf_op jit(solution)/shard_map/dot_general | solution.py:67
  39.9 0.0 copy-done.2
  39.9 1.5 %collective-permute-start = (bf16[128,1024]{1,0:T(8,128)(2,1)S(1)}, bf16[128,1024]{1,0:T(8,128)(2,1)S(1)}, u32[]{:S(2)}, u32[]{:S(2)}) collective-permute-start(bf16[128,1024]{1,0:T(8,128)(2,1)S(1)} %fusion.12), channel_id=1, source_target_pairs={{0,4},{4,0},{8,12},{12,8},{16,20},{20,16},{24,28},{28,24},{1,5},{5... | collective-permute-start | bytes 786440 | tf_op jit(solution)/shard_map/ppermute | solution.py:12
  41.4 0.8 constant_dynamic-slice_fusion.1
  42.2 5.4 %all-gather = bf16[1,256,256]{2,1,0:T(8,128)(2,1)S(1)} all-gather(bf16[1,64,256]{2,1,0:T(8,128)(2,1)S(1)} %constant_dynamic-slice_fusion.1), channel_id=2, replica_groups=mesh['leaf'=8,'rhs'=4] {'rhs'}, dimensions={1}, use_global_device_ids=true | all-gather | bytes 163840 | tf_op jit(solution)/shard_map/all_gather | solution.py:61
  47.6 0.8 collective-permute-done
  48.4 0.0 copy-done.4
  48.4 2.9 %fusion.13 = f32[1024,1024]{0,1:T(8,128)} fusion(bf16[128,1024]{1,0:T(8,128)(2,1)S(1)} %collective-permute-done, bf16[128,1024]{1,0:T(8,128)(2,1)S(1)} %fusion.12, pred[]{:T(512)S(6)} %eq.19, bf16[3,1024,128]{2,1,0:T(8,128)(2,1)S(1)} %copy-done.4, bf16[1,256,256]{2,1,0:T(8,128)(2,1)S(1)} %all-gather, s32[]{:T(128)S(6)} %select_n.93), kind=kOutput, calls=%fused_computation.14 | convolution fusion | flops 338034688 | bytes 5046277 | tf_op jit(solution)/shard_map/dot_general | solution.py:77
  51.3 3.4 %fusion.9 = f32[128,1024]{1,0:T(8,128)S(1)} fusion(f32[1024,1024]{0,1:T(8,128)} %fusion.13, bf16[1024,1024]{1,0:T(8,128)(2,1)} %copy-done.2, bf16[3,1024,128]{2,1,0:T(8,128)(2,1)} %param.9), kind=kOutput, calls=%fused_computation.10 | convolution fusion | flops 271581184 | bytes 7077888 | tf_op jit(solution)/shard_map/dot_general | solution.py:67
  54.7 0.7 slice_select_fusion.1
  55.4 1.5 %collective-permute-start.1 = (f32[128,512]{1,0:T(8,128)}, f32[128,512]{1,0:T(8,128)}, u32[]{:S(2)}, u32[]{:S(2)}) collective-permute-start(f32[128,512]{1,0:T(8,128)} %slice_select_fusion.1), channel_id=1, source_target_pairs={{0,4},{4,0},{8,12},{12,8},{16,20},{20,16},{24,28},{28,24},{1,5},{5... | collective-permute-start | bytes 786440 | tf_op jit(solution)/shard_map/ppermute | solution.py:12
  56.9 6.6 %collective-permute-done.1 = f32[128,512]{1,0:T(8,128)} collective-permute-done((f32[128,512]{1,0:T(8,128)}, f32[128,512]{1,0:T(8,128)}, u32[]{:S(2)}, u32[]{:S(2)}) %collective-permute-start.1) | collective-permute-done | bytes 262176 | tf_op jit(solution)/shard_map/ppermute | solution.py:12
  63.5 1.0 add_convert_fusion
  64.5 1.6 %collective-permute-start.2 = (bf16[128,512]{1,0:T(8,128)(2,1)S(1)}, bf16[128,512]{1,0:T(8,128)(2,1)S(1)}, u32[]{:S(2)}, u32[]{:S(2)}) collective-permute-start(bf16[128,512]{1,0:T(8,128)(2,1)S(1)} %add_convert_fusion), channel_id=1, source_target_pairs={{0,8},{4,12},{8,0},{12,4},{16,24},{20,28},{24,16},{28,20},{1,9},{5... | collective-permute-start | bytes 393224 | tf_op jit(solution)/shard_map/ppermute | solution.py:12
  66.1 0.0 copy-done.6
  66.1 5.4 %all-gather.1 = bf16[1,256,256]{2,1,0:T(8,128)(2,1)S(1)} all-gather(bf16[1,64,256]{2,1,0:T(8,128)(2,1)S(1)} %constant_dynamic-slice_fusion), channel_id=3, replica_groups=mesh['leaf'=8,'rhs'=4] {'rhs'}, dimensions={1}, use_global_device_ids=true | all-gather | bytes 163840 | tf_op jit(solution)/shard_map/all_gather | solution.py:62
  71.5 0.0 collective-permute-done.2
  71.5 0.2 convolution_convert_fusion.3
  71.7 1.4 %collective-permute-start.3 = (bf16[128,512]{1,0:T(8,128)(2,1)S(1)}, bf16[128,512]{1,0:T(8,128)(2,1)S(1)}, u32[]{:S(2)}, u32[]{:S(2)}) collective-permute-start(bf16[128,512]{1,0:T(8,128)(2,1)S(1)} %convolution_convert_fusion.3), channel_id=1, source_target_pairs={{0,4},{4,0},{8,12},{12,8},{16,20},{20,16},{24,28},{28,24},{1,5},{5... | collective-permute-start | bytes 393224 | tf_op jit(solution)/shard_map/ppermute | solution.py:12
  73.1 4.4 %collective-permute-done.3 = bf16[128,512]{1,0:T(8,128)(2,1)S(1)} collective-permute-done((bf16[128,512]{1,0:T(8,128)(2,1)S(1)}, bf16[128,512]{1,0:T(8,128)(2,1)S(1)}, u32[]{:S(2)}, u32[]{:S(2)}) %collective-permute-start.3) | collective-permute-done | bytes 131104 | tf_op jit(solution)/shard_map/ppermute | solution.py:12
  77.5 0.0 copy-done.3
  77.5 2.9 %bitcast_subtract_fusion.1 = f32[1024,1024]{1,0:T(8,128)S(1)} fusion(f32[1024,1024]{0,1:T(8,128)} %fusion.13, bf16[1024,1024]{1,0:T(8,128)(2,1)S(1)} %copy-done.3, bf16[128,512]{1,0:T(8,128)(2,1)S(1)} %convolution_convert_fusion.3, bf16[128,512]{1,0:T(8,128)(2,1)S(1)} %collective-permute-done.3, bf16[3,1024,128]{2,1,0:T(8,128)(2,1)S(1)} %copy-done.4, ...), kind=kOutput, calls=%fused_computation.2 | convolution fusion | flops 272760832 | bytes 11010049 | tf_op jit(solution)/shard_map/dot_general | solution.py:77
  80.5 0.0 copy-start.1
  80.5 1.6 %fusion.6 = f32[128,1024]{1,0:T(8,128)S(1)} fusion(f32[1024,1024]{1,0:T(8,128)S(1)} %bitcast_subtract_fusion.1, bf16[3,1024,128]{2,1,0:T(8,128)(2,1)} %param.9), kind=kOutput, calls=%fused_computation.9 | convolution fusion | flops 269484032 | bytes 4980736 | tf_op jit(solution)/shard_map/dot_general | solution.py:67
  82.1 0.3 copy-done.1
  82.4 0.7 slice_select_fusion
  83.2 1.3 %collective-permute-start.4 = (f32[128,512]{1,0:T(8,128)}, f32[128,512]{1,0:T(8,128)}, u32[]{:S(2)}, u32[]{:S(2)}) collective-permute-start(f32[128,512]{1,0:T(8,128)} %slice_select_fusion), channel_id=1, source_target_pairs={{0,4},{4,0},{8,12},{12,8},{16,20},{20,16},{24,28},{28,24},{1,5},{5... | collective-permute-start | bytes 786440 | tf_op jit(solution)/shard_map/ppermute | solution.py:12
  84.5 6.7 %collective-permute-done.4 = f32[128,512]{1,0:T(8,128)} collective-permute-done((f32[128,512]{1,0:T(8,128)}, f32[128,512]{1,0:T(8,128)}, u32[]{:S(2)}, u32[]{:S(2)}) %collective-permute-start.4) | collective-permute-done | bytes 262176 | tf_op jit(solution)/shard_map/ppermute | solution.py:12
  91.2 1.0 select_add_fusion
  92.2 0.6 collective-permute-start.5
  92.8 4.4 %collective-permute-done.5 = f32[128,256]{1,0:T(8,128)S(1)} collective-permute-done((f32[128,256]{1,0:T(8,128)S(1)}, f32[128,256]{1,0:T(8,128)S(1)}, u32[]{:S(2)}, u32[]{:S(2)}) %collective-permute-start.5) | collective-permute-done | bytes 131104 | tf_op jit(solution)/shard_map/ppermute | solution.py:12
  97.3 3.2 %collective-permute-start.6 = (bf16[128,256]{1,0:T(8,128)(2,1)S(1)}, bf16[128,256]{1,0:T(8,128)(2,1)S(1)}, u32[]{:S(2)}, u32[]{:S(2)}) collective-permute-start(bf16[128,256]{1,0:T(8,128)(2,1)S(1)} %add_convert_fusion.1), channel_id=1, source_target_pairs={{0,16},{4,20},{8,24},{12,28},{16,0},{20,4},{24,8},{28,12},{1,17},{... | collective-permute-start | bytes 196616 | tf_op jit(solution)/shard_map/ppermute | solution.py:12
  100.5 5.4 %all-gather.2 = bf16[1,256,256]{2,1,0:T(8,128)(2,1)S(1)} all-gather(bf16[1,64,256]{2,1,0:T(8,128)(2,1)S(1)} %copy-done.5), channel_id=4, replica_groups=mesh['leaf'=8,'rhs'=4] {'rhs'}, dimensions={1}, use_global_device_ids=true | all-gather | bytes 163840 | tf_op jit(solution)/shard_map/all_gather | solution.py:63
  105.9 0.0 collective-permute-done.6
  105.9 0.2 convolution_convert_fusion.4
  106.0 0.1 collective-permute-start.7
  106.1 4.3 %collective-permute-done.7 = bf16[128,256]{1,0:T(8,128)(2,1)S(1)} collective-permute-done((bf16[128,256]{1,0:T(8,128)(2,1)S(1)}, bf16[128,256]{1,0:T(8,128)(2,1)S(1)}, u32[]{:S(2)}, u32[]{:S(2)}) %collective-permute-start.7) | collective-permute-done | bytes 65568 | tf_op jit(solution)/shard_map/ppermute | solution.py:12
  110.5 1.4 %collective-permute-start.8 = (bf16[128,512]{1,0:T(8,128)(2,1)S(1)}, bf16[128,512]{1,0:T(8,128)(2,1)S(1)}, u32[]{:S(2)}, u32[]{:S(2)}) collective-permute-start(bf16[128,512]{1,0:T(8,128)(2,1)S(1)} %maximum_select_fusion.11), channel_id=1, source_target_pairs={{0,4},{4,0},{8,12},{12,8},{16,20},{20,16},{24,28},{28,24},{1,5},{5... | collective-permute-start | bytes 393224 | tf_op jit(solution)/shard_map/ppermute | solution.py:12
  111.8 3.7 %collective-permute-done.8 = bf16[128,512]{1,0:T(8,128)(2,1)S(1)} collective-permute-done((bf16[128,512]{1,0:T(8,128)(2,1)S(1)}, bf16[128,512]{1,0:T(8,128)(2,1)S(1)}, u32[]{:S(2)}, u32[]{:S(2)}) %collective-permute-start.8) | collective-permute-done | bytes 131104 | tf_op jit(solution)/shard_map/ppermute | solution.py:12
  115.5 4.2 %fusion = bf16[1024,1024]{1,0:T(8,128)(2,1)} fusion(f32[1024,1024]{1,0:T(8,128)} %copy-done.1, bf16[128,512]{1,0:T(8,128)(2,1)S(1)} %maximum_select_fusion.11, bf16[128,512]{1,0:T(8,128)(2,1)S(1)} %collective-permute-done.8, bf16[3,1024,128]{2,1,0:T(8,128)(2,1)S(1)} %copy-done.4, pred[]{:T(512)S(6)} %eq.20), kind=kOutput, calls=%fused_computation.1 | convolution fusion | flops 271712256 | bytes 6815745 | tf_op jit(solution)/shard_map/dot_general | solution.py:77
  (8 shorter events, 0.1 us)
Async XLA Ops:
  6.5 27.7 %copy-start = (bf16[1024,1024]{1,0:T(8,128)(2,1)S(1)}, bf16[1024,1024]{1,0:T(8,128)(2,1)}, u32[]{:S(2)}) copy-start(bf16[1024,1024]{1,0:T(8,128)(2,1)} %param.7) | copy-start | bytes 6291460
  6.5 27.7 %all-gather.5.cloned.1.call-start = ((), (), s32[]{:S(2)}) async-start(), calls=%async_computation | async-start | bytes 2621440 | tf_op jit(solution)/shard_map/all_gather | solution.py:52
  38.1 1.8 %copy-start.2 = (bf16[1024,1024]{1,0:T(8,128)(2,1)}, bf16[1024,1024]{1,0:T(8,128)(2,1)S(1)}, u32[]{:S(2)}) copy-start(bf16[1024,1024]{1,0:T(8,128)(2,1)S(1)} %convolution_convert_fusion) | copy-start | bytes 6291460
  38.2 10.3 %copy-start.4 = (bf16[3,1024,128]{2,1,0:T(8,128)(2,1)S(1)}, bf16[3,1024,128]{2,1,0:T(8,128)(2,1)}, u32[]{:S(2)}) copy-start(bf16[3,1024,128]{2,1,0:T(8,128)(2,1)} %param.10) | copy-start | bytes 2359300
  39.9 8.5 %collective-permute-start = (bf16[128,1024]{1,0:T(8,128)(2,1)S(1)}, bf16[128,1024]{1,0:T(8,128)(2,1)S(1)}, u32[]{:S(2)}, u32[]{:S(2)}) collective-permute-start(bf16[128,1024]{1,0:T(8,128)(2,1)S(1)} %fusion.12), channel_id=1, source_target_pairs={{0,4},{4,0},{8,12},{12,8},{16,20},{20,16},{24,28},{28,24},{1,5},{5... | collective-permute-start | bytes 786440 | tf_op jit(solution)/shard_map/ppermute | solution.py:12
  51.3 14.8 %copy-start.6 = (bf16[2,64,256]{2,1,0:T(8,128)(2,1)S(1)}, bf16[2,64,256]{2,1,0:T(8,128)(2,1)}, u32[]{:S(2)}) copy-start(bf16[2,64,256]{2,1,0:T(8,128)(2,1)} %param.12) | copy-start | bytes 196612
  55.4 8.1 %collective-permute-start.1 = (f32[128,512]{1,0:T(8,128)}, f32[128,512]{1,0:T(8,128)}, u32[]{:S(2)}, u32[]{:S(2)}) collective-permute-start(f32[128,512]{1,0:T(8,128)} %slice_select_fusion.1), channel_id=1, source_target_pairs={{0,4},{4,0},{8,12},{12,8},{16,20},{20,16},{24,28},{28,24},{1,5},{5... | collective-permute-start | bytes 786440 | tf_op jit(solution)/shard_map/ppermute | solution.py:12
  56.9 20.6 %copy-start.3 = (bf16[1024,1024]{1,0:T(8,128)(2,1)S(1)}, bf16[1024,1024]{1,0:T(8,128)(2,1)}, u32[]{:S(2)}) copy-start(bf16[1024,1024]{1,0:T(8,128)(2,1)} %copy-done.2) | copy-start | bytes 6291460
  64.5 7.0 %collective-permute-start.2 = (bf16[128,512]{1,0:T(8,128)(2,1)S(1)}, bf16[128,512]{1,0:T(8,128)(2,1)S(1)}, u32[]{:S(2)}, u32[]{:S(2)}) collective-permute-start(bf16[128,512]{1,0:T(8,128)(2,1)S(1)} %add_convert_fusion), channel_id=1, source_target_pairs={{0,8},{4,12},{8,0},{12,4},{16,24},{20,28},{24,16},{28,20},{1,9},{5... | collective-permute-start | bytes 393224 | tf_op jit(solution)/shard_map/ppermute | solution.py:12
  71.7 5.8 %collective-permute-start.3 = (bf16[128,512]{1,0:T(8,128)(2,1)S(1)}, bf16[128,512]{1,0:T(8,128)(2,1)S(1)}, u32[]{:S(2)}, u32[]{:S(2)}) collective-permute-start(bf16[128,512]{1,0:T(8,128)(2,1)S(1)} %convolution_convert_fusion.3), channel_id=1, source_target_pairs={{0,4},{4,0},{8,12},{12,8},{16,20},{20,16},{24,28},{28,24},{1,5},{5... | collective-permute-start | bytes 393224 | tf_op jit(solution)/shard_map/ppermute | solution.py:12
  80.5 2.0 %copy-start.1 = (f32[1024,1024]{1,0:T(8,128)}, f32[1024,1024]{1,0:T(8,128)S(1)}, u32[]{:S(2)}) copy-start(f32[1024,1024]{1,0:T(8,128)S(1)} %bitcast_subtract_fusion.1) | copy-start | bytes 12582916
  82.4 18.0 %copy-start.5 = (bf16[1,64,256]{2,1,0:T(8,128)(2,1)S(1)}, bf16[1,64,256]{2,1,0:T(8,128)(2,1)}, u32[]{:S(2)}) copy-start(bf16[1,64,256]{2,1,0:T(8,128)(2,1)} %param.13) | copy-start | bytes 98308
  83.2 8.0 %collective-permute-start.4 = (f32[128,512]{1,0:T(8,128)}, f32[128,512]{1,0:T(8,128)}, u32[]{:S(2)}, u32[]{:S(2)}) collective-permute-start(f32[128,512]{1,0:T(8,128)} %slice_select_fusion), channel_id=1, source_target_pairs={{0,4},{4,0},{8,12},{12,8},{16,20},{20,16},{24,28},{28,24},{1,5},{5... | collective-permute-start | bytes 786440 | tf_op jit(solution)/shard_map/ppermute | solution.py:12
  92.2 5.0 %collective-permute-start.5 = (f32[128,256]{1,0:T(8,128)S(1)}, f32[128,256]{1,0:T(8,128)S(1)}, u32[]{:S(2)}, u32[]{:S(2)}) collective-permute-start(f32[128,256]{1,0:T(8,128)S(1)} %slice_select_fusion.2), channel_id=1, source_target_pairs={{0,8},{4,12},{8,0},{12,4},{16,24},{20,28},{24,16},{28,20},{1,9},{5... | collective-permute-start | bytes 393224 | tf_op jit(solution)/shard_map/ppermute | solution.py:12
  97.3 8.6 %collective-permute-start.6 = (bf16[128,256]{1,0:T(8,128)(2,1)S(1)}, bf16[128,256]{1,0:T(8,128)(2,1)S(1)}, u32[]{:S(2)}, u32[]{:S(2)}) collective-permute-start(bf16[128,256]{1,0:T(8,128)(2,1)S(1)} %add_convert_fusion.1), channel_id=1, source_target_pairs={{0,16},{4,20},{8,24},{12,28},{16,0},{20,4},{24,8},{28,12},{1,17},{... | collective-permute-start | bytes 196616 | tf_op jit(solution)/shard_map/ppermute | solution.py:12
  106.0 4.4 %collective-permute-start.7 = (bf16[128,256]{1,0:T(8,128)(2,1)S(1)}, bf16[128,256]{1,0:T(8,128)(2,1)S(1)}, u32[]{:S(2)}, u32[]{:S(2)}) collective-permute-start(bf16[128,256]{1,0:T(8,128)(2,1)S(1)} %convolution_convert_fusion.4), channel_id=1, source_target_pairs={{0,8},{4,12},{8,0},{12,4},{16,24},{20,28},{24,16},{28,20},{1,9},{5... | collective-permute-start | bytes 196616 | tf_op jit(solution)/shard_map/ppermute | solution.py:12
  110.5 5.0 %collective-permute-start.8 = (bf16[128,512]{1,0:T(8,128)(2,1)S(1)}, bf16[128,512]{1,0:T(8,128)(2,1)S(1)}, u32[]{:S(2)}, u32[]{:S(2)}) collective-permute-start(bf16[128,512]{1,0:T(8,128)(2,1)S(1)} %maximum_select_fusion.11), channel_id=1, source_target_pairs={{0,4},{4,0},{8,12},{12,8},{16,20},{20,16},{24,28},{28,24},{1,5},{5... | collective-permute-start | bytes 393224 | tf_op jit(solution)/shard_map/ppermute | solution.py:12
Sparse Core Ops, SparseCore 0:
  8.9 25.2 all-gather.4
where the time goes:
time: 127 us
  waiting for transfers between devices  58.6 us (46%)
  matrix products  21.1 us (17%)
  blocking collectives  16.2 us (13%)
  between operations  13.5 us (11%)
  starting transfers between devices  12.5 us (10%)
  other arithmetic  3.56 us (3%)
    ppermute x9, waiting for transfers between devices, from_partner(): return lax.ppermute(value, axis, pairs)  31 us
    all_gather x1, waiting for transfers between devices, local(): lax.all_gather(leaf_inverse, 'rhs', axis=0, tiled=True)  27 us
    ppermute x9, starting transfers between devices, from_partner(): return lax.ppermute(value, axis, pairs)  12.5 us
    dot_general x3, matrix products, local(): jnp.dot(correct_factors[level], answer, preferred_element_type=jnp.float32)  10 us
    dot_general x3, matrix products, local(): jnp.dot(project_factors[level].T, rounded, preferred_element_type=jnp.flo...  6.76 us
    all_gather x1, blocking collectives, local(): lax.all_gather(own_nodes[1], 'rhs', axis=0, tiled=True)  5.4 us
    all_gather x1, blocking collectives, local(): lax.all_gather(own_nodes[2], 'rhs', axis=0, tiled=True)  5.4 us
    all_gather x1, blocking collectives, local(): lax.all_gather(own_nodes[0], 'rhs', axis=0, tiled=True)  5.4 us
  transfers between devices with their start and end apart: 10, of which 8 were waited for; matrix products, arithmetic and copies ran while one was open for 1% of the time, Pallas kernels for 0%

commit v1 on v0

v1 whole, which is shorter than its diff:
```python
import functools

import jax
import jax.numpy as jnp
from jax import lax
from jax.experimental import pallas as pl
from jax.experimental.pallas import tpu as pltpu
from jax.sharding import PartitionSpec as P

LEVELS = 3
CHUNKS = 4
BF = jnp.bfloat16
F32 = jnp.float32


def mm(a, b):
    return jnp.dot(a, b, preferred_element_type=F32)


def mmt(a, b):
    return lax.dot_general(a, b, (((0,), (0,)), ((), ())), preferred_element_type=F32)


def bit_of(index, stride):
    return lax.rem(lax.div(index, stride), 2)


def flip(index, stride):
    return index + stride * (1 - 2 * bit_of(index, stride))


def kernel(
    b_hbm, a_hbm, p_hbm, c_hbm, w0_hbm, w1_hbm, w2_hbm, out_hbm,
    b_v, a_v, p_v, c_v, w_v, g_v, qf, q_s, q_r, q_v,
    p0_s, p0_r, p1f, p1_s, p1_r, s1_s, s1_r, p2f, p2_s, p2_r,
    s2_s, s2_r, t2_s, t2_r, a_cat, start, out_v,
    lsem, osem, ssem, rsem,
):
    i = lax.axis_index("leaf")
    r = lax.axis_index("rhs")
    blk = a_hbm.shape[0]
    depth = a_hbm.shape[1]
    rows = b_hbm.shape[0]
    cols = b_hbm.shape[1]
    rank = p_hbm.shape[2]
    cw = cols // CHUNKS
    half = depth // 2
    mate = {"rhs": flip(r, 1)}
    across = {"rhs": flip(r, 2)}
    sib = {"leaf": flip(i, 1)}
    near = {"leaf": flip(i, 2)}
    far = {"leaf": flip(i, 4)}
    sides = [bit_of(i, 1), bit_of(i, 2), bit_of(i, 4)]
    core = bit_of(r, 1)
    chip = bit_of(r, 2)

    count = [0]
    copies = []

    def send(src, dst, to):
        k = count[0]
        count[0] += 1
        copy = pltpu.make_async_remote_copy(
            src_ref=src, dst_ref=dst, send_sem=ssem.at[k], recv_sem=rsem.at[k],
            device_id=to, device_id_type=pl.DeviceIdType.MESH,
        )
        copy.start()
        copies.append(copy)
        return copy

    nloc = [0]

    def fetch(src, dst):
        copy = pltpu.make_async_copy(src, dst, lsem.at[nloc[0]])
        nloc[0] += 1
        copy.start()
        return copy

    def block(which):
        return pl.ds(pl.multiple_of(which * blk, blk), blk)

    la = fetch(a_hbm, a_v.at[block(r), :])
    lw = [
        fetch(w_hbm.at[lax.div(i, 2 << level)], w_v.at[level, r])
        for level, w_hbm in enumerate((w0_hbm, w1_hbm, w2_hbm))
    ]
    lp = [fetch(p_hbm.at[l], p_v.at[:, pl.ds(l * rank, rank)]) for l in range(LEVELS)]
    lc = [fetch(c_hbm.at[l], c_v.at[:, pl.ds(l * rank, rank)]) for l in range(LEVELS)]
    lb = fetch(b_hbm, b_v)

    barrier = pltpu.get_barrier_semaphore()
    for to in (mate, across, sib, near, far):
        pl.semaphore_signal(barrier, inc=1, device_id=to, device_id_type=pl.DeviceIdType.MESH)
    pl.semaphore_wait(barrier, 5)

    la.wait()
    a_mate = send(a_v.at[block(r), :], a_v.at[block(r), :], mate)
    for copy in lw:
        copy.wait()
    w_across = send(w_v.at[:, r], w_v.at[:, r], across)
    w_mate = send(w_v.at[:, r], w_v.at[:, r], mate)
    for copy in lp:
        copy.wait()
    for copy in lc:
        copy.wait()
    a_mate.wait_recv()
    pair_rows = pl.ds(pl.multiple_of(chip * 2 * blk, 2 * blk), 2 * blk)
    half_cols = pl.ds(pl.multiple_of(core * half, half), half)
    q_across = []
    for l in range(LEVELS):
        part = mmt(p_v[pair_rows, pl.ds(l * rank, rank)], a_v[pair_rows, half_cols])
        qf[l] = part
        q_s[l] = part.astype(BF)
        q_across.append(send(q_s.at[l], q_r.at[l], across))
    pieces = 4
    piece = blk // pieces

    def piece_rows(which, k):
        return pl.ds(pl.multiple_of(which * blk + k * piece, piece), piece)

    a_across = [
        send(a_v.at[piece_rows(r, k), :], a_v.at[piece_rows(r, k), :], across)
        for k in range(pieces)
    ]
    for n, (l, k) in enumerate(((1, 0), (2, 0), (2, 1))):
        g_v[n] = mmt(p_v[:, pl.ds(l * rank, rank)], c_v[:, pl.ds(k * rank, rank)]).astype(BF)
    w_across.wait_recv()
    w_relay = send(w_v.at[:, flip(r, 2)], w_v.at[:, flip(r, 2)], mate)
    lb.wait()

    def finish_q(l):
        q_across[l].wait_recv()
        q_v[l, core] = (qf[l] + q_r[l].astype(F32)).astype(BF)
        return send(q_v.at[l, core], q_v.at[l, core], mate)

    def project(l, c):
        own = pl.ds(c * cw, cw)
        return mm(q_v[l, 0], b_v[pl.ds(0, half), own]) + mm(q_v[l, 1], b_v[pl.ds(half, half), own])

    def start_rows(which):
        for c in range(CHUNKS):
            own = pl.ds(c * cw, cw)
            start[block(which), own] = mm(a_v[block(which), :], b_v[:, own]).astype(BF)

    def weight(l, other):
        row = pl.ds(pl.multiple_of(sides[l] * 2, 2), 2)
        column = (1 - sides[l]) if other else sides[l]
        lanes = pl.ds(pl.multiple_of(column * rank, rank), rank)
        return w_v[l, row, :, lanes].reshape(rank, rank)

    q_mate = [finish_q(0)]
    q_mate[0].wait_recv()
    x0 = []
    for c in range(CHUNKS):
        p0_s[c] = project(0, c).astype(BF)
        x0.append(send(p0_s.at[c], p0_r.at[c], sib))
    q_mate.append(finish_q(1))
    start_rows(r)
    q_mate[1].wait_recv()
    for c in range(CHUNKS):
        p1f[c] = project(1, c)
    w_mate.wait_recv()
    w_relay.wait_recv()
    x1 = []
    for c in range(CHUNKS):
        x0[c].wait_recv()
        a0 = (mm(weight(0, False), p0_s[c]) + mm(weight(0, True), p0_r[c])).astype(BF)
        a_cat[c, pl.ds(0, rank), :] = a0
        part = p1f[c] - mm(g_v[0], a0)
        p1f[c] = part
        p1_s[c] = part.astype(BF)
        x1.append(send(p1_s.at[c], p1_r.at[c], sib))
    q_mate.append(finish_q(2))
    start_rows(flip(r, 1))
    q_mate[2].wait_recv()
    for c in range(CHUNKS):
        p2f[c] = project(2, c) - mm(g_v[1], a_cat[c, pl.ds(0, rank), :])
    z1 = []
    relay = []

    def relay_piece(k):
        a_across[k].wait_recv()
        where = piece_rows(flip(r, 2), k)
        relay.append(send(a_v.at[where, :], a_v.at[where, :], mate))

    for c in range(CHUNKS):
        x1[c].wait_recv()
        s1_s[c] = (p1f[c] + p1_r[c].astype(F32)).astype(BF)
        z1.append(send(s1_s.at[c], s1_r.at[c], near))
    x2 = []
    for c in range(CHUNKS):
        z1[c].wait_recv()
        a1 = (mm(weight(1, False), s1_s[c]) + mm(weight(1, True), s1_r[c])).astype(BF)
        a_cat[c, pl.ds(rank, rank), :] = a1
        part = p2f[c] - mm(g_v[2], a1)
        p2f[c] = part
        p2_s[c] = part.astype(BF)
        x2.append(send(p2_s.at[c], p2_r.at[c], sib))
    for k in range(pieces):
        relay_piece(k)
    n1 = []
    for c in range(CHUNKS):
        x2[c].wait_recv()
        p2f[c] = p2f[c] + p2_r[c].astype(F32)
        if c % 2 == 1:
            j = c // 2
            s2_s[j] = p2f[2 * j + 1 - sides[1]].astype(BF)
            n1.append(send(s2_s.at[j], s2_r.at[j], near))
    start_rows(flip(r, 2))
    f1 = []
    for j in range(CHUNKS // 2):
        n1[j].wait_recv()
        t2_s[j] = (p2f[2 * j + sides[1]] + s2_r[j].astype(F32)).astype(BF)
        f1.append(send(t2_s.at[j], t2_r.at[j], far))
    for copy in relay:
        copy.wait_recv()
    start_rows(flip(flip(r, 2), 1))
    n2 = []
    for j in range(CHUNKS // 2):
        f1[j].wait_recv()
        mine = 2 * j + sides[1]
        where = pl.ds(2 * rank, rank)
        a_cat[mine, where, :] = (
            mm(weight(2, False), t2_s[j]) + mm(weight(2, True), t2_r[j])
        ).astype(BF)
        n2.append(send(a_cat.at[mine, where, :], a_cat.at[mine, where, :], near))
    outs = []
    for c in range(CHUNKS):
        if c % 2 == 0:
            n2[c // 2].wait_recv()
        own = pl.ds(c * cw, cw)
        for n in range(4):
            band = pl.ds(n * (rows // 4), rows // 4)
            out_v[band, own] = (start[band, own].astype(F32) - mm(c_v[band, :], a_cat[c])).astype(BF)
        copy = pltpu.make_async_copy(out_v.at[:, own], out_hbm.at[:, own], osem.at[c])
        copy.start()
        outs.append(copy)
    for copy in copies:
        copy.wait_send()
    for copy in outs:
        copy.wait()


def local(right_sides, leaf_inverse, project_factors, correct_factors, *couplings):
    rows, cols = right_sides.shape
    blk, depth = leaf_inverse.shape
    levels, _, rank = project_factors.shape
    parts = lax.axis_size("rhs")
    cw = cols // CHUNKS
    full = lambda dtype: pltpu.VMEM((CHUNKS, rank, cw), dtype)
    part = lambda dtype: pltpu.VMEM((CHUNKS // 2, rank, cw), dtype)
    copies = 64
    any_spec = pl.BlockSpec(memory_space=pl.ANY)
    return pl.pallas_call(
        kernel,
        out_shape=jax.ShapeDtypeStruct((rows, cols), BF),
        in_specs=[any_spec] * 7,
        out_specs=any_spec,
        scratch_shapes=[
            pltpu.VMEM((rows, cols), BF),
            pltpu.VMEM((rows, depth), BF),
            pltpu.VMEM((rows, levels * rank), BF),
            pltpu.VMEM((rows, levels * rank), BF),
            pltpu.VMEM((levels, parts) + couplings[0].shape[1:], BF),
            pltpu.VMEM((3, rank, rank), BF),
            pltpu.VMEM((levels, rank, depth // 2), F32),
            pltpu.VMEM((levels, rank, depth // 2), BF),
            pltpu.VMEM((levels, rank, depth // 2), BF),
            pltpu.VMEM((levels, 2, rank, depth // 2), BF),
            full(BF), full(BF), full(F32), full(BF), full(BF), full(BF), full(BF),
            full(F32), full(BF), full(BF),
            part(BF), part(BF), part(BF), part(BF),
            pltpu.VMEM((CHUNKS, levels * rank, cw), BF),
            pltpu.VMEM((rows, cols), BF),
            pltpu.VMEM((rows, cols), BF),
            pltpu.SemaphoreType.DMA((16,)),
            pltpu.SemaphoreType.DMA((CHUNKS,)),
            pltpu.SemaphoreType.DMA((copies,)),
            pltpu.SemaphoreType.DMA((copies,)),
        ],
        compiler_params=pltpu.CompilerParams(
            collective_id=0, has_side_effects=True, vmem_limit_bytes=48 * 1024 * 1024
        ),
    )(right_sides, leaf_inverse, project_factors, correct_factors, *couplings)


def solution(mesh):
    in_specs = (
        P("leaf", "rhs"),
        P(("leaf", "rhs"), None),
        P(None, "leaf", None),
        P(None, "leaf", None),
        P(None, "rhs", None),
        P(None, "rhs", None),
        P(None, "rhs", None),
    )
    out_specs = P("leaf", "rhs")
    return jax.shard_map(local, mesh=mesh, in_specs=in_specs, out_specs=out_specs, check_vma=False)
```

time: 127 us -> 56.4 us (0.44)
  waiting for transfers between devices: 58.6 us -> 0 us
  Pallas kernels: 0 us -> 48.8 us
  matrix products: 21.1 us -> 0 us
  blocking collectives: 16.2 us -> 0 us
  between operations: 13.5 us -> 0.02 us
  starting transfers between devices: 12.5 us -> 0 us
  local copies, waits for them, and re-layouts: 1.1 us -> 7.13 us
  other arithmetic: 3.56 us -> 0 us
    pallas_call x0 -> x1, Pallas kernels: none -> 48.8 us  [local(): pl.pallas_call(kernel, out_shape=jax.ShapeDtypeStruct((rows, cols), BF),...]
    ppermute x9 -> x0, waiting for transfers between devices: 31 us -> none  [from_partner(): return lax.ppermute(value, axis, pairs)]
    all_gather x1 -> x0, waiting for transfers between devices: 27 us -> none  [local(): lax.all_gather(leaf_inverse, 'rhs', axis=0, tiled=True)]
    dot_general x9 -> x0, matrix products: 21.1 us -> none  [the longest x3 10 us: local(): jnp.dot(correct_factors[level], answer, preferred_element_type=jnp.float32)]
    all_gather x3 -> x0, blocking collectives: 16.2 us -> none  [the longest x1 5.4 us: local(): lax.all_gather(own_nodes[1], 'rhs', axis=0, tiled=True)]
    ppermute x9 -> x0, starting transfers between devices: 12.5 us -> none  [from_partner(): return lax.ppermute(value, axis, pairs)]
    unnamed x14 -> x13, local copies, waits for them, and re-layouts: 0.33 us -> 7.13 us
    select_n x4 -> x0, other arithmetic: 1.53 us -> none  [the longest x3 1.5 us: halve(): outgoing = jnp.where(upper_side, lower, higher)]
  transfers between devices with their start and end apart: 10 -> 0, of which waited for: 8 -> 0; matrix products, arithmetic and copies ran while one was open for 1% -> 0% of each run, Pallas kernels for 0% -> 0%
where the time goes in v1:
time: 56.4 us; the launch traced here: 56 us
  Pallas kernels  48.8 us (87%)
  local copies, waits for them, and re-layouts  7.13 us (13%)
    pallas_call x1, Pallas kernels, local(): pl.pallas_call(kernel, out_shape=jax.ShapeDtypeStruct((rows, cols), BF),...  48.8 us
    unnamed x13, local copies, waits for them, and re-layouts  7.13 us

profile of v1, /device:TPU:0, one launch (start us, length us, event | category | flops | bytes accessed | tf_op | source)
XLA Modules:
  0.0 56.0 jit_solution(8778823419489235680)
XLA Ops:
  0.0 0.0 copy-start
  0.0 1.1 %copy-done = bf16[3,1024,128]{2,1,0:T(8,128)(2,1)S(1)} copy-done((bf16[3,1024,128]{2,1,0:T(8,128)(2,1)S(1)}, bf16[3,1024,128]{2,1,0:T(8,128)(2,1)}, u32[]{:S(2)}) %copy-start) | copy-done | bytes 786456
  1.1 0.0 copy-start.1
  1.1 1.1 %copy-done.1 = bf16[3,1024,128]{2,1,0:T(8,128)(2,1)S(1)} copy-done((bf16[3,1024,128]{2,1,0:T(8,128)(2,1)S(1)}, bf16[3,1024,128]{2,1,0:T(8,128)(2,1)}, u32[]{:S(2)}) %copy-start.1) | copy-done | bytes 786456
  2.3 0.0 copy-start.2
  2.3 1.0 %copy-done.2 = bf16[256,1024]{1,0:T(8,128)(2,1)S(1)} copy-done((bf16[256,1024]{1,0:T(8,128)(2,1)S(1)}, bf16[256,1024]{1,0:T(8,128)(2,1)}, u32[]{:S(2)}) %copy-start.2) | copy-done | bytes 524312
  3.3 0.0 copy-start.3
  3.3 0.9 %copy-done.3 = bf16[4,64,256]{2,1,0:T(8,128)(2,1)S(1)} copy-done((bf16[4,64,256]{2,1,0:T(8,128)(2,1)S(1)}, bf16[4,64,256]{2,1,0:T(8,128)(2,1)}, u32[]{:S(2)}) %copy-start.3) | copy-done | bytes 131096
  4.2 0.0 copy-start.4
  4.2 0.8 %copy-done.4 = bf16[2,64,256]{2,1,0:T(8,128)(2,1)S(1)} copy-done((bf16[2,64,256]{2,1,0:T(8,128)(2,1)S(1)}, bf16[2,64,256]{2,1,0:T(8,128)(2,1)}, u32[]{:S(2)}) %copy-start.4) | copy-done | bytes 65560
  5.1 0.0 copy-start.5
  5.1 0.8 %copy-done.5 = bf16[1,64,256]{2,1,0:T(8,128)(2,1)S(1)} copy-done((bf16[1,64,256]{2,1,0:T(8,128)(2,1)S(1)}, bf16[1,64,256]{2,1,0:T(8,128)(2,1)}, u32[]{:S(2)}) %copy-start.5) | copy-done | bytes 32792
  5.8 48.8 %shard_map.73 = bf16[1024,1024]{1,0:T(8,128)(2,1)S(1)} custom-call(bf16[1024,1024]{1,0:T(8,128)(2,1)} %b_hbm.1, bf16[256,1024]{1,0:T(8,128)(2,1)S(1)} %copy-done.2, bf16[3,1024,128]{2,1,0:T(8,128)(2,1)S(1)} %copy-done, bf16[3,1024,128]{2,1,0:T(8,128)(2,1)S(1)} %copy-done.1, bf16[4,64,256]{2,1,0:T(8,128)(2,1)S(1)} %copy-done.3, ...), custom_call_target="tpu_custom_call" | custom-call | tf_op jit(solution)/shard_map/pallas_call | solution.py:254
  54.7 1.3 %copy.9 = bf16[1024,1024]{1,0:T(8,128)(2,1)} copy(bf16[1024,1024]{1,0:T(8,128)(2,1)S(1)} %shard_map.73) | data formatting | bytes 4194304
Async XLA Ops:
  0.0 1.1 %copy-start = (bf16[3,1024,128]{2,1,0:T(8,128)(2,1)S(1)}, bf16[3,1024,128]{2,1,0:T(8,128)(2,1)}, u32[]{:S(2)}) copy-start(bf16[3,1024,128]{2,1,0:T(8,128)(2,1)} %p_hbm.1) | copy-start | bytes 2359300
  1.1 1.1 %copy-start.1 = (bf16[3,1024,128]{2,1,0:T(8,128)(2,1)S(1)}, bf16[3,1024,128]{2,1,0:T(8,128)(2,1)}, u32[]{:S(2)}) copy-start(bf16[3,1024,128]{2,1,0:T(8,128)(2,1)} %c_hbm.1) | copy-start | bytes 2359300
  2.3 1.0 %copy-start.2 = (bf16[256,1024]{1,0:T(8,128)(2,1)S(1)}, bf16[256,1024]{1,0:T(8,128)(2,1)}, u32[]{:S(2)}) copy-start(bf16[256,1024]{1,0:T(8,128)(2,1)} %a_hbm.1) | copy-start | bytes 1572868
  3.3 0.9 %copy-start.3 = (bf16[4,64,256]{2,1,0:T(8,128)(2,1)S(1)}, bf16[4,64,256]{2,1,0:T(8,128)(2,1)}, u32[]{:S(2)}) copy-start(bf16[4,64,256]{2,1,0:T(8,128)(2,1)} %w0_hbm.1) | copy-start | bytes 393220
  4.2 0.8 %copy-start.4 = (bf16[2,64,256]{2,1,0:T(8,128)(2,1)S(1)}, bf16[2,64,256]{2,1,0:T(8,128)(2,1)}, u32[]{:S(2)}) copy-start(bf16[2,64,256]{2,1,0:T(8,128)(2,1)} %w1_hbm.1) | copy-start | bytes 196612
  5.1 0.8 %copy-start.5 = (bf16[1,64,256]{2,1,0:T(8,128)(2,1)S(1)}, bf16[1,64,256]{2,1,0:T(8,128)(2,1)}, u32[]{:S(2)}) copy-start(bf16[1,64,256]{2,1,0:T(8,128)(2,1)} %w2_hbm.1) | copy-start | bytes 98308

commit v2 on v1

--- a/solution.py
+++ b/solution.py
@@ -30,11 +30,11 @@
 
 
 def kernel(
-    b_hbm, a_hbm, p_hbm, c_hbm, w0_hbm, w1_hbm, w2_hbm, out_hbm,
+    b_hbm, a_hbm, p_hbm, c_hbm, w0_hbm, w1_hbm, w2_hbm, out_v,
     b_v, a_v, p_v, c_v, w_v, g_v, qf, q_s, q_r, q_v,
     p0_s, p0_r, p1f, p1_s, p1_r, s1_s, s1_r, p2f, p2_s, p2_r,
-    s2_s, s2_r, t2_s, t2_r, a_cat, start, out_v,
-    lsem, osem, ssem, rsem,
+    s2_s, s2_r, t2_s, t2_r, a_cat, start,
+    lsem, ssem, rsem,
 ):
     i = lax.axis_index("leaf")
     r = lax.axis_index("rhs")
@@ -224,7 +224,6 @@
             mm(weight(2, False), t2_s[j]) + mm(weight(2, True), t2_r[j])
         ).astype(BF)
         n2.append(send(a_cat.at[mine, where, :], a_cat.at[mine, where, :], near))
-    outs = []
     for c in range(CHUNKS):
         if c % 2 == 0:
             n2[c // 2].wait_recv()
@@ -232,13 +231,8 @@
         for n in range(4):
             band = pl.ds(n * (rows // 4), rows // 4)
             out_v[band, own] = (start[band, own].astype(F32) - mm(c_v[band, :], a_cat[c])).astype(BF)
-        copy = pltpu.make_async_copy(out_v.at[:, own], out_hbm.at[:, own], osem.at[c])
-        copy.start()
-        outs.append(copy)
     for copy in copies:
         copy.wait_send()
-    for copy in outs:
-        copy.wait()
 
 
 def local(right_sides, leaf_inverse, project_factors, correct_factors, *couplings):
@@ -250,12 +244,12 @@
     full = lambda dtype: pltpu.VMEM((CHUNKS, rank, cw), dtype)
     part = lambda dtype: pltpu.VMEM((CHUNKS // 2, rank, cw), dtype)
     copies = 64
-    any_spec = pl.BlockSpec(memory_space=pl.ANY)
+    any_spec = pl.BlockSpec(memory_space=pltpu.HBM)
     return pl.pallas_call(
         kernel,
         out_shape=jax.ShapeDtypeStruct((rows, cols), BF),
         in_specs=[any_spec] * 7,
-        out_specs=any_spec,
+        out_specs=pl.BlockSpec(memory_space=pltpu.VMEM),
         scratch_shapes=[
             pltpu.VMEM((rows, cols), BF),
             pltpu.VMEM((rows, depth), BF),
@@ -272,16 +266,17 @@
             part(BF), part(BF), part(BF), part(BF),
             pltpu.VMEM((CHUNKS, levels * rank, cw), BF),
             pltpu.VMEM((rows, cols), BF),
-            pltpu.VMEM((rows, cols), BF),
             pltpu.SemaphoreType.DMA((16,)),
-            pltpu.SemaphoreType.DMA((CHUNKS,)),
             pltpu.SemaphoreType.DMA((copies,)),
             pltpu.SemaphoreType.DMA((copies,)),
         ],
         compiler_params=pltpu.CompilerParams(
             collective_id=0, has_side_effects=True, vmem_limit_bytes=48 * 1024 * 1024
         ),
-    )(right_sides, leaf_inverse, project_factors, correct_factors, *couplings)
+    )(*(
+        pltpu.with_memory_space_constraint(x, pltpu.HBM)
+        for x in (right_sides, leaf_inverse, project_factors, correct_factors, *couplings)
+    ))
 
 
 def solution(mesh):

time: 56.4 us -> 49.5 us (0.88)
  local copies, waits for them, and re-layouts: 7.13 us -> 1.32 us
  Pallas kernels: 48.8 us -> 48.1 us
    unnamed x13 -> x1, local copies, waits for them, and re-layouts: 7.13 us -> 1.32 us
    pallas_call x1, Pallas kernels: 48.8 us -> 48.1 us  [local(): pl.pallas_call(kernel, out_shape=jax.ShapeDtypeStruct((rows, cols), BF),...]
where the time goes in v2:
time: 49.5 us; the launch traced here: 49.4 us
  Pallas kernels  48.1 us (97%)
  local copies, waits for them, and re-layouts  1.32 us (3%)
    pallas_call x1, Pallas kernels, local(): pl.pallas_call(kernel, out_shape=jax.ShapeDtypeStruct((rows, cols), BF),...  48.1 us
    unnamed x1, local copies, waits for them, and re-layouts  1.32 us

profile of v2, /device:TPU:0, one launch (start us, length us, event | category | flops | bytes accessed | tf_op | source)
XLA Modules:
  0.0 49.4 jit_solution(14311199872349577272)
XLA Ops:
  0.0 48.1 %shard_map.73 = bf16[1024,1024]{1,0:T(8,128)(2,1)S(1)} custom-call(bf16[1024,1024]{1,0:T(8,128)(2,1)} %b_hbm.1, bf16[256,1024]{1,0:T(8,128)(2,1)} %a_hbm.1, bf16[3,1024,128]{2,1,0:T(8,128)(2,1)} %p_hbm.1, bf16[3,1024,128]{2,1,0:T(8,128)(2,1)} %c_hbm.1, bf16[4,64,256]{2,1,0:T(8,128)(2,1)} %w0_hbm.1, bf16[2,64,256]{2,1,0:T(8,128)(2,1)} %w1_hbm.1, ...), custom_call_target="tpu_custom_call" | custom-call | tf_op jit(solution)/shard_map/pallas_call | solution.py:248
  48.1 1.3 %copy.9 = bf16[1024,1024]{1,0:T(8,128)(2,1)} copy(bf16[1024,1024]{1,0:T(8,128)(2,1)S(1)} %shard_map.73) | data formatting | bytes 4194304

commit v3 on v2

v3 whole, which is shorter than its diff:
```python
import functools

import jax
import jax.numpy as jnp
from jax import lax
from jax.experimental import pallas as pl
from jax.experimental.pallas import tpu as pltpu
from jax.sharding import PartitionSpec as P

LEVELS = 3
CHUNKS = 4
BF = jnp.bfloat16
F32 = jnp.float32


def mm(a, b):
    return jnp.dot(a, b, preferred_element_type=F32)


def bit_of(index, stride):
    return lax.rem(lax.div(index, stride), 2)


def flip(index, stride):
    return index + stride * (1 - 2 * bit_of(index, stride))


def kernel(
    b_hbm, a_hbm, p_hbm, c_hbm, w0_hbm, w1_hbm, w2_hbm, out_v,
    b_v, a_v, p_v, pt_v, c_v, w_v, g_v, qf, q_s, q_r, q_v,
    stack, p0f, p0_s, p0_r, p1f, p1_s, p1_r, s1_s, s1_r, p2f, p2_s, p2_r,
    s2_s, s2_r, t2_s, t2_r, a_cat, start,
    lsem, ssem, rsem,
):
    i = lax.axis_index("leaf")
    r = lax.axis_index("rhs")
    blk = a_hbm.shape[0]
    depth = a_hbm.shape[1]
    rows = b_hbm.shape[0]
    cols = b_hbm.shape[1]
    rank = p_hbm.shape[2]
    cw = cols // CHUNKS
    half = depth // 2
    mate = {"rhs": flip(r, 1)}
    across = {"rhs": flip(r, 2)}
    sib = {"leaf": flip(i, 1)}
    near = {"leaf": flip(i, 2)}
    far = {"leaf": flip(i, 4)}
    diag = {"leaf": flip(flip(i, 1), 2)}
    sides = [bit_of(i, 1), bit_of(i, 2), bit_of(i, 4)]
    core = bit_of(r, 1)
    chip = bit_of(r, 2)

    count = [0]
    copies = []

    def send(src, dst, to):
        k = count[0]
        count[0] += 1
        copy = pltpu.make_async_remote_copy(
            src_ref=src, dst_ref=dst, send_sem=ssem.at[k], recv_sem=rsem.at[k],
            device_id=to, device_id_type=pl.DeviceIdType.MESH,
        )
        copy.start()
        copies.append(copy)
        return copy

    nloc = [0]

    def fetch(src, dst):
        copy = pltpu.make_async_copy(src, dst, lsem.at[nloc[0]])
        nloc[0] += 1
        copy.start()
        return copy

    def block(which):
        return pl.ds(pl.multiple_of(which * blk, blk), blk)

    la = fetch(a_hbm, a_v.at[block(r), :])
    lw = [
        fetch(w_hbm.at[lax.div(i, 2 << level)], w_v.at[level, r])
        for level, w_hbm in enumerate((w0_hbm, w1_hbm, w2_hbm))
    ]
    lp = [fetch(p_hbm.at[l], p_v.at[:, pl.ds(l * rank, rank)]) for l in range(LEVELS)]
    lc = [fetch(c_hbm.at[l], c_v.at[:, pl.ds(l * rank, rank)]) for l in range(LEVELS)]
    lb = fetch(b_hbm, b_v)

    barrier = pltpu.get_barrier_semaphore()
    for to in (mate, across, sib, near, far, diag):
        pl.semaphore_signal(barrier, inc=1, device_id=to, device_id_type=pl.DeviceIdType.MESH)
    for l in range(LEVELS):
        lp[l].wait()
        pt_v[l] = p_v[:, pl.ds(l * rank, rank)].T
    pl.semaphore_wait(barrier, 6)

    la.wait()
    half_cols = pl.ds(pl.multiple_of(core * half, half), half)
    rest_cols = pl.ds(pl.multiple_of((1 - core) * half, half), half)
    a_mate = send(a_v.at[block(r), rest_cols], a_v.at[block(r), rest_cols], mate)
    a_mate2 = send(a_v.at[block(r), half_cols], a_v.at[block(r), half_cols], mate)
    for copy in lw:
        copy.wait()
    w_across = [send(w_v.at[0, r], w_v.at[0, r], across)]
    w_mate = send(w_v.at[:, r], w_v.at[:, r], mate)
    a_mate.wait_recv()
    pair_rows = pl.ds(pl.multiple_of(chip * 2 * blk, 2 * blk), 2 * blk)
    q_across = []
    for l in range(LEVELS):
        part = mm(pt_v[l, :, pair_rows], a_v[pair_rows, half_cols])
        qf[l] = part
        q_s[l] = part.astype(BF)
        q_across.append(send(q_s.at[l], q_r.at[l], across))
    for l in range(1, LEVELS):
        w_across.append(send(w_v.at[l, r], w_v.at[l, r], across))
    pieces = 4
    piece = blk // pieces

    def piece_rows(which, k):
        return pl.ds(pl.multiple_of(which * blk + k * piece, piece), piece)

    a_across = [
        send(a_v.at[piece_rows(r, k), :], a_v.at[piece_rows(r, k), :], across)
        for k in range(pieces)
    ]
    for copy in lc:
        copy.wait()
    own_lanes = pl.ds(pl.multiple_of(sides[0] * rank, rank), rank)
    g_send = []
    for n, (l, k) in enumerate(((1, 0), (2, 0), (2, 1))):
        g_v[n, :, own_lanes] = mm(pt_v[l], c_v[:, pl.ds(k * rank, rank)]).astype(BF)
        g_send.append(send(g_v.at[n, :, own_lanes], g_v.at[n, :, own_lanes], sib))

    def relay_w(l):
        w_across[l].wait_recv()
        w_relay.append(send(w_v.at[l, flip(r, 2)], w_v.at[l, flip(r, 2)], mate))

    w_relay = []
    relay_w(0)
    lb.wait()

    def finish_q(l):
        q_across[l].wait_recv()
        q_v[l, core] = (qf[l] + q_r[l].astype(F32)).astype(BF)
        return send(q_v.at[l, core], q_v.at[l, core], mate)

    def project(l, c):
        own = pl.ds(c * cw, cw)
        return mm(q_v[l, 0], b_v[pl.ds(0, half), own]) + mm(q_v[l, 1], b_v[pl.ds(half, half), own])

    def start_rows(which):
        for c in range(CHUNKS):
            own = pl.ds(c * cw, cw)
            start[block(which), own] = mm(a_v[block(which), :], b_v[:, own]).astype(BF)

    def weight(l, other):
        row = pl.ds(pl.multiple_of(sides[l] * 2, 2), 2)
        column = (1 - sides[l]) if other else sides[l]
        lanes = pl.ds(pl.multiple_of(column * rank, rank), rank)
        return w_v[l, row, :, lanes].reshape(rank, rank)

    hw = cw // 2
    keep = pl.ds(pl.multiple_of(sides[0] * hw, hw), hw)
    give = pl.ds(pl.multiple_of((1 - sides[0]) * hw, hw), hw)
    exchange = []
    for l, (f_v, s_v, r_v) in enumerate(((p0f, p0_s, p0_r), (p1f, p1_s, p1_r), (p2f, p2_s, p2_r))):
        copy = finish_q(l)
        if l == 2:
            a_mate2.wait_recv()
            start_rows(r)
        copy.wait_recv()
        sends = []
        for c in range(CHUNKS):
            part = project(l, c)
            if l > 0:
                f_v[c] = part
            if l < 2:
                s_v[c] = part.astype(BF)
            else:
                s_v[c] = f_v[c, :, give].astype(BF)
            sends.append(send(s_v.at[c], r_v.at[c], sib))
        exchange.append(sends)
    x0, x1, x2 = exchange
    w_mate.wait_recv()
    w_relay[0].wait_recv()
    for copy in g_send:
        copy.wait_recv()
    mine_rows = pl.ds(pl.multiple_of(sides[0] * rank, rank), rank)
    other_rows = pl.ds(pl.multiple_of((1 - sides[0]) * rank, rank), rank)
    node = w_v[0].reshape(2 * rank, 2 * rank)

    def first(c):
        x0[c].wait_recv()
        stack[c, mine_rows, :] = p0_s[c]
        stack[c, other_rows, :] = p0_r[c]
        both = mm(node, stack[c]).astype(BF)
        stack[c] = both
        a_cat[c, pl.ds(0, rank), :] = stack[c, mine_rows, :]
        p1f[c] = p1f[c] - mm(g_v[0], both)
        p2f[c, :, keep] = p2f[c, :, keep] - mm(g_v[1], stack[c, :, keep])

    z1 = []

    def second_sum(c):
        x1[c].wait_recv()
        s1_s[c] = (p1f[c] + p1_r[c].astype(F32)).astype(BF)
        z1.append(send(s1_s.at[c], s1_r.at[c], near))

    def second(c):
        z1[c].wait_recv()
        a1 = (mm(weight(1, False), s1_s[c]) + mm(weight(1, True), s1_r[c])).astype(BF)
        a_cat[c, pl.ds(rank, rank), :] = a1
        a1 = a_cat[c, pl.ds(rank, rank), keep]
        p2f[c, :, keep] = (
            p2f[c, :, keep] - mm(g_v[2, :, pl.ds(0, rank)], a1) - mm(g_v[2, :, pl.ds(rank, rank)], a1)
        )

    n1 = []

    def third_sum(c):
        x2[c].wait_recv()
        p2f[c, :, keep] = p2f[c, :, keep] + p2_r[c].astype(F32)
        if c % 2 == 1:
            j = c // 2
            s2_s[j] = p2f[2 * j + 1 - sides[1], :, keep].astype(BF)
            n1.append(send(s2_s.at[j], s2_r.at[j], near))

    f1 = []

    def third_far(j):
        n1[j].wait_recv()
        t2_s[j] = (p2f[2 * j + sides[1], :, keep] + s2_r[j].astype(F32)).astype(BF)
        f1.append(send(t2_s.at[j], t2_r.at[j], far))

    n2 = []

    def third(j):
        f1[j].wait_recv()
        mine = 2 * j + sides[1]
        where = pl.ds(2 * rank, rank)
        a_cat[mine, where, keep] = (
            mm(weight(2, False), t2_s[j]) + mm(weight(2, True), t2_r[j])
        ).astype(BF)
        spot = a_cat.at[mine, where, keep]
        n2.append([send(spot, spot, to) for to in (diag, sib, near)])

    relay = []

    def relay_piece(k):
        a_across[k].wait_recv()
        where = piece_rows(flip(r, 2), k)
        relay.append(send(a_v.at[where, :], a_v.at[where, :], mate))

    def finish(c):
        own = pl.ds(c * cw, cw)
        for n in range(4):
            band = pl.ds(n * (rows // 4), rows // 4)
            out_v[band, own] = (start[band, own].astype(F32) - mm(c_v[band, :], a_cat[c])).astype(BF)

    relay_w(1)
    relay_w(2)
    start_rows(flip(r, 1))
    for c in range(CHUNKS):
        first(c)
    for c in range(CHUNKS):
        second_sum(c)
        if c == 1:
            w_relay[1].wait_recv()
            w_relay[2].wait_recv()
    lag = CHUNKS // 2
    for c in range(lag):
        second(c)
    for c in range(CHUNKS):
        if c + lag < CHUNKS:
            second(c + lag)
        third_sum(c)
    for k in range(pieces):
        relay_piece(k)
    for j in range(CHUNKS // 2):
        third_far(j)
    start_rows(flip(r, 2))
    for copy in relay:
        copy.wait_recv()
    start_rows(flip(flip(r, 2), 1))
    for j in range(CHUNKS // 2):
        third(j)
    for j in range(CHUNKS // 2):
        for copy in n2[j]:
            copy.wait_recv()
        finish(2 * j)
        finish(2 * j + 1)
    for copy in copies:
        copy.wait_send()


def local(right_sides, leaf_inverse, project_factors, correct_factors, *couplings):
    rows, cols = right_sides.shape
    blk, depth = leaf_inverse.shape
    levels, _, rank = project_factors.shape
    parts = lax.axis_size("rhs")
    cw = cols // CHUNKS
    full = lambda dtype: pltpu.VMEM((CHUNKS, rank, cw), dtype)
    thin = lambda dtype: pltpu.VMEM((CHUNKS, rank, cw // 2), dtype)
    part = lambda dtype: pltpu.VMEM((CHUNKS // 2, rank, cw // 2), dtype)
    copies = 96
    any_spec = pl.BlockSpec(memory_space=pltpu.HBM)
    return pl.pallas_call(
        kernel,
        out_shape=jax.ShapeDtypeStruct((rows, cols), BF),
        in_specs=[any_spec] * 7,
        out_specs=pl.BlockSpec(memory_space=pltpu.VMEM),
        scratch_shapes=[
            pltpu.VMEM((rows, cols), BF),
            pltpu.VMEM((rows, depth), BF),
            pltpu.VMEM((rows, levels * rank), BF),
            pltpu.VMEM((levels, rank, rows), BF),
            pltpu.VMEM((rows, levels * rank), BF),
            pltpu.VMEM((levels, parts) + couplings[0].shape[1:], BF),
            pltpu.VMEM((3, rank, 2 * rank), BF),
            pltpu.VMEM((levels, rank, depth // 2), F32),
            pltpu.VMEM((levels, rank, depth // 2), BF),
            pltpu.VMEM((levels, rank, depth // 2), BF),
            pltpu.VMEM((levels, 2, rank, depth // 2), BF),
            pltpu.VMEM((CHUNKS, 2 * rank, cw), BF),
            full(F32), full(BF), full(BF), full(F32), full(BF), full(BF), full(BF), full(BF),
            full(F32), thin(BF), thin(BF),
            part(BF), part(BF), part(BF), part(BF),
            pltpu.VMEM((CHUNKS, levels * rank, cw), BF),
            pltpu.VMEM((rows, cols), BF),
            pltpu.SemaphoreType.DMA((16,)),
            pltpu.SemaphoreType.DMA((copies,)),
            pltpu.SemaphoreType.DMA((copies,)),
        ],
        compiler_params=pltpu.CompilerParams(
            collective_id=0, has_side_effects=True, vmem_limit_bytes=48 * 1024 * 1024
        ),
    )(*(
        pltpu.with_memory_space_constraint(x, pltpu.HBM)
        for x in (right_sides, leaf_inverse, project_factors, correct_factors, *couplings)
    ))


def solution(mesh):
    in_specs = (
        P("leaf", "rhs"),
        P(("leaf", "rhs"), None),
        P(None, "leaf", None),
        P(None, "leaf", None),
        P(None, "rhs", None),
        P(None, "rhs", None),
        P(None, "rhs", None),
    )
    out_specs = P("leaf", "rhs")
    return jax.shard_map(local, mesh=mesh, in_specs=in_specs, out_specs=out_specs, check_vma=False)
```

time: 49.5 us -> 46 us (0.929)
  Pallas kernels: 48.1 us -> 44.5 us
    pallas_call x1, Pallas kernels: 48.1 us -> 44.5 us  [local(): pl.pallas_call(kernel, out_shape=jax.ShapeDtypeStruct((rows, cols), BF),...]
where the time goes in v3:
time: 46 us; the launch traced here: 45.9 us
  Pallas kernels  44.5 us (97%)
  local copies, waits for them, and re-layouts  1.32 us (3%)
    pallas_call x1, Pallas kernels, local(): pl.pallas_call(kernel, out_shape=jax.ShapeDtypeStruct((rows, cols), BF),...  44.5 us
    unnamed x1, local copies, waits for them, and re-layouts  1.32 us

profile of v3, /device:TPU:0, one launch (start us, length us, event | category | flops | bytes accessed | tf_op | source)
XLA Modules:
  0.0 45.9 jit_solution(17386018355794265123)
XLA Ops:
  0.0 44.5 %shard_map.73 = bf16[1024,1024]{1,0:T(8,128)(2,1)S(1)} custom-call(bf16[1024,1024]{1,0:T(8,128)(2,1)} %b_hbm.1, bf16[256,1024]{1,0:T(8,128)(2,1)} %a_hbm.1, bf16[3,1024,128]{2,1,0:T(8,128)(2,1)} %p_hbm.1, bf16[3,1024,128]{2,1,0:T(8,128)(2,1)} %c_hbm.1, bf16[4,64,256]{2,1,0:T(8,128)(2,1)} %w0_hbm.1, bf16[2,64,256]{2,1,0:T(8,128)(2,1)} %w1_hbm.1, ...), custom_call_target="tpu_custom_call" | custom-call | tf_op jit(solution)/shard_map/pallas_call | solution.py:306
  44.5 1.3 %copy.9 = bf16[1024,1024]{1,0:T(8,128)(2,1)} copy(bf16[1024,1024]{1,0:T(8,128)(2,1)S(1)} %shard_map.73) | data formatting | bytes 4194304

commit v4 on v3

--- a/solution.py
+++ b/solution.py
@@ -88,9 +88,8 @@
     barrier = pltpu.get_barrier_semaphore()
     for to in (mate, across, sib, near, far, diag):
         pl.semaphore_signal(barrier, inc=1, device_id=to, device_id_type=pl.DeviceIdType.MESH)
-    for l in range(LEVELS):
-        lp[l].wait()
-        pt_v[l] = p_v[:, pl.ds(l * rank, rank)].T
+    lp[0].wait()
+    pt_v[0] = p_v[:, pl.ds(0, rank)].T
     pl.semaphore_wait(barrier, 6)
 
     la.wait()
@@ -106,6 +105,9 @@
     pair_rows = pl.ds(pl.multiple_of(chip * 2 * blk, 2 * blk), 2 * blk)
     q_across = []
     for l in range(LEVELS):
+        if l > 0:
+            lp[l].wait()
+            pt_v[l] = p_v[:, pl.ds(l * rank, rank)].T
         part = mm(pt_v[l, :, pair_rows], a_v[pair_rows, half_cols])
         qf[l] = part
         q_s[l] = part.astype(BF)
@@ -266,16 +268,17 @@
         if c == 1:
             w_relay[1].wait_recv()
             w_relay[2].wait_recv()
-    lag = CHUNKS // 2
-    for c in range(lag):
+    second(0)
+    second(1)
+    third_sum(0)
+    third_sum(1)
+    for c in range(2, CHUNKS):
         second(c)
-    for c in range(CHUNKS):
-        if c + lag < CHUNKS:
-            second(c + lag)
         third_sum(c)
+    third_far(0)
     for k in range(pieces):
         relay_piece(k)
-    for j in range(CHUNKS // 2):
+    for j in range(1, CHUNKS // 2):
         third_far(j)
     start_rows(flip(r, 2))
     for copy in relay:

time: 46 us -> 45.1 us (0.980)
  Pallas kernels: 44.5 us -> 43.6 us
    pallas_call x1, Pallas kernels: 44.5 us -> 43.6 us  [local(): pl.pallas_call(kernel, out_shape=jax.ShapeDtypeStruct((rows, cols), BF),...]
where the time goes in v4:
time: 45.1 us; the launch traced here: 44.9 us
  Pallas kernels  43.6 us (97%)
  local copies, waits for them, and re-layouts  1.32 us (3%)
    pallas_call x1, Pallas kernels, local(): pl.pallas_call(kernel, out_shape=jax.ShapeDtypeStruct((rows, cols), BF),...  43.6 us
    unnamed x1, local copies, waits for them, and re-layouts  1.32 us

profile of v4, /device:TPU:0, one launch (start us, length us, event | category | flops | bytes accessed | tf_op | source)
XLA Modules:
  0.0 44.9 jit_solution(14080758983143520459)
XLA Ops:
  0.0 43.6 %shard_map.73 = bf16[1024,1024]{1,0:T(8,128)(2,1)S(1)} custom-call(bf16[1024,1024]{1,0:T(8,128)(2,1)} %b_hbm.1, bf16[256,1024]{1,0:T(8,128)(2,1)} %a_hbm.1, bf16[3,1024,128]{2,1,0:T(8,128)(2,1)} %p_hbm.1, bf16[3,1024,128]{2,1,0:T(8,128)(2,1)} %c_hbm.1, bf16[4,64,256]{2,1,0:T(8,128)(2,1)} %w0_hbm.1, bf16[2,64,256]{2,1,0:T(8,128)(2,1)} %w1_hbm.1, ...), custom_call_target="tpu_custom_call" | custom-call | tf_op jit(solution)/shard_map/pallas_call | solution.py:309
  43.6 1.3 %copy.9 = bf16[1024,1024]{1,0:T(8,128)(2,1)} copy(bf16[1024,1024]{1,0:T(8,128)(2,1)S(1)} %shard_map.73) | data formatting | bytes 4194304
